TPU v7x, 32 devices: a whole 2x2x4 slice. The times are simulated.
32 devices in a mesh: dp: 8 (over y, x, core), fsdp: 4 (over z).
Axes of the slice: x: 2, y: 2, z: 4, core: 2. Of those that a mesh axis runs over, the one named last changes fastest.
Arguments:
- grads: float32 [32, 96, 128], P(('dp', 'fsdp')), may hold values from -0.6 to 0.6
- last_peak: float32 [96], replicated, may hold values from 0.05 to 0.8
- master: float32 [96, 128], P(('dp', 'fsdp')), may hold values from -6 to 6
- moment1: float32 [96, 128], P(('dp', 'fsdp')), may hold values from -6 to 6
- moment2: float32 [96, 128], P(('dp', 'fsdp')), may hold values from 0.25 to 8
Outputs:
- new_master: float32 [96, 128], P(('dp', 'fsdp'))
- new_moment1: float32 [96, 128], P(('dp', 'fsdp'))
- new_moment2: float32 [96, 128], P(('dp', 'fsdp'))
- weights: bfloat16 [96, 128], replicated
- block_peak: float32 [96], replicated
All inputs are finite; a program needn't handle non-finite values.
Results may differ from a plain program's by a relative error of at most 0.0035.
Values may be sent and summed in bfloat16 or wider, within the bound.
No kernel may reach another device: no remote copies, remote signals or barrier semaphores. Data moves between devices by JAX's collectives and lax.ppermute only.
A program may use at most 64 MiB of HBM per device.

v0:
```python
import jax
import jax.numpy as jnp
from jax import lax
from jax.sharding import PartitionSpec as P

STEP_COUNT = 10
code_limit = 448.0
peak_floor = 0.05
beta_one = 0.9
beta_two = 0.95
learn_rate = 0.05
decay_rate = 0.1
epsilon = 1e-08


def quantize(rows, inverse):
    codes = jnp.clip(rows * inverse[:, None], -code_limit, code_limit).astype(jnp.bfloat16)
    return lax.optimization_barrier(codes).astype(jnp.float32)


def adamw(gradient, master, moment1, moment2):
    first = beta_one * moment1 + (1.0 - beta_one) * gradient
    second = beta_two * moment2 + (1.0 - beta_two) * gradient * gradient
    corrected_one = first / (1.0 - beta_one**STEP_COUNT)
    corrected_two = second / (1.0 - beta_two**STEP_COUNT)
    updated = master - learn_rate * (
        corrected_one / (jnp.sqrt(corrected_two) + epsilon) + decay_rate * master
    )
    return (updated, first, second)


def body(grads, last_peak, master, moment1, moment2):
    local = grads[0]
    peak = lax.pmax(jnp.max(jnp.abs(local), axis=1), ("dp", "fsdp"))
    floored = jnp.maximum(last_peak, peak_floor)
    inverse = code_limit / floored
    scale = floored / code_limit
    owned = master.shape[0]
    first_row = lax.axis_index(("dp", "fsdp")) * owned
    summed = lax.psum_scatter(
        quantize(local, inverse), ("dp", "fsdp"), scatter_dimension=0, tiled=True
    )
    own_scale = lax.dynamic_slice_in_dim(scale, first_row, owned, 0)
    gradient = summed * own_scale[:, None]
    updated, first, second = adamw(gradient, master, moment1, moment2)
    rounded = updated.astype(jnp.bfloat16)
    grouped_rows = lax.all_gather(rounded, "fsdp", axis=0, tiled=True)
    weights = lax.all_gather(grouped_rows, "dp", axis=0, tiled=True)
    return (updated, first, second, weights, peak)


def solution(mesh):
    placed = (
        P(("dp", "fsdp"), None, None),
        P(),
        P(("dp", "fsdp"), None),
        P(("dp", "fsdp"), None),
        P(("dp", "fsdp"), None),
    )
    return jax.shard_map(
        body,
        mesh=mesh,
        in_specs=placed,
        out_specs=(
            P(("dp", "fsdp"), None),
            P(("dp", "fsdp"), None),
            P(("dp", "fsdp"), None),
            P(),
            P(),
        ),
        check_vma=False,
    )
```

profile of v0, /device:TPU:12, one launch (start us, length us, event | category | flops | bytes accessed | tf_op | source)
XLA Modules:
  0.0 103.9 jit_solution(240758746087156561)
XLA Ops:
  0.6 0.0 copy-start.3
  0.6 0.6 copy-done.3
  1.3 0.1 dynamic_slice.3
  1.4 1.0 fusion.2
  2.4 41.5 %all-reduce = f32[96,128]{1,0:T(8,128)S(1)} all-reduce(bf16[96,128]{1,0:T(8,128)(2,1)S(1)} %get-tuple-element.10), channel_id=2, replica_groups=mesh['dp'=8,'fsdp'=4] {'dp','fsdp'}, use_global_device_ids=true, to_apply=%region_0.0.clone | all-reduce | flops 12288 | bytes 73728
  43.9 0.0 copy-start.2
  43.9 0.0 copy-start
  43.9 0.0 copy-start.1
  43.9 0.6 copy-done.2
  44.6 0.0 copy-done
  44.6 0.0 copy-done.1
  44.6 0.7 convert_bitcast_fusion
  45.3 8.1 %all-gather = bf16[4,3,128]{2,1,0:T(4,128)(2,1)S(1)} all-gather(bf16[1,3,128]{2,1,0:T(4,128)(2,1)S(1)} %get-tuple-element.5), channel_id=1, replica_groups=mesh['dp'=8,'fsdp'=4] {'fsdp'}, dimensions={0}, use_global_device_ids=true | all-gather | bytes 3840 | tf_op jit(solution)/shard_map/all_gather | solution.py:47
  53.4 8.1 %all-gather.1 = bf16[8,12,128]{2,1,0:T(8,128)(2,1)S(1)} all-gather(bf16[1,12,128]{2,1,0:T(8,128)(2,1)S(1)} %reshape.14), channel_id=1, replica_groups=mesh['dp'=8,'fsdp'=4] {'dp'}, dimensions={0}, use_global_device_ids=true | all-gather | bytes 27648 | tf_op jit(solution)/shard_map/all_gather | solution.py:48
  61.5 0.6 reshape.15
  62.1 41.7 %pmax.7 = f32[96]{0:T(128)} all-reduce(f32[96]{0:T(128)S(1)} %get-tuple-element.9), channel_id=1, replica_groups=mesh['dp'=8,'fsdp'=4] {'dp','fsdp'}, use_global_device_ids=true, to_apply=%region_2.3 | all-reduce | flops 96 | bytes 768 | tf_op jit(solution)/shard_map/pmax | solution.py:34
  (2 shorter events, 0.0 us)
Async XLA Ops:
  0.6 0.7 copy-start.3
  43.9 0.7 copy-start.2
  43.9 0.7 copy-start
  43.9 0.7 copy-start.1
where the time goes:
time: 104 us
  blocking collectives  99.5 us (96%)
  local copies, waits for them, and re-layouts  2.05 us (2%)
  other arithmetic  1.66 us (2%)
    pmax x1, blocking collectives, body(): peak = lax.pmax(jnp.max(jnp.abs(local), axis=1), ('dp', 'fsdp'))  41.7 us
    unnamed x1, blocking collectives  41.5 us
    all_gather x1, blocking collectives, body(): weights = lax.all_gather(grouped_rows, 'dp', axis=0, tiled=True)  8.11 us
    all_gather x1, blocking collectives, body(): grouped_rows = lax.all_gather(rounded, 'fsdp', axis=0, tiled=True)  8.08 us

commit v1 on v0

--- a/solution.py
+++ b/solution.py
@@ -45,7 +45,12 @@
     updated, first, second = adamw(gradient, master, moment1, moment2)
     rounded = updated.astype(jnp.bfloat16)
     grouped_rows = lax.all_gather(rounded, "fsdp", axis=0, tiled=True)
-    weights = lax.all_gather(grouped_rows, "dp", axis=0, tiled=True)
+    ring = [grouped_rows]
+    for hop in range(7):
+        ring.append(lax.ppermute(ring[-1], "dp", [(dev, (dev + 1) % 8) for dev in range(8)]))
+    weights = jnp.roll(
+        jnp.concatenate(ring[::-1], axis=0), (lax.axis_index("dp") + 1) * ring[0].shape[0], axis=0
+    )
     return (updated, first, second, weights, peak)
 
 

time: 104 us -> 121 us (1.16)
  waiting for transfers between devices: 0 us -> 23.6 us
  blocking collectives: 99.5 us -> 91.4 us
    ppermute x0 -> x7, waiting for transfers between devices: none -> 23.6 us  [body(): lax.ppermute(ring[-1], 'dp', [(dev, (dev + 1) % 8) for dev in range(8)])]
    all_gather x1 -> x0, blocking collectives: 8.11 us -> none  [body(): weights = lax.all_gather(grouped_rows, 'dp', axis=0, tiled=True)]
  transfers between devices with their start and end apart: 0 -> 7, of which waited for: 0 -> 6; matrix products, arithmetic and copies ran while one was open for 0% -> 0% of each run, Pallas kernels for 0% -> 0%
where the time goes in v1:
time: 121 us; the launch traced here: 120 us
  blocking collectives  91.4 us (76%)
  waiting for transfers between devices  23.6 us (20%)
  local copies, waits for them, and re-layouts  2.91 us (2%)
  other arithmetic  1.66 us (1%)
    pmax x1, blocking collectives, body(): peak = lax.pmax(jnp.max(jnp.abs(local), axis=1), ('dp', 'fsdp'))  41.8 us
    unnamed x1, blocking collectives  41.5 us
    ppermute x7, waiting for transfers between devices, body(): lax.ppermute(ring[-1], 'dp', [(dev, (dev + 1) % 8) for dev in range(8)])  23.6 us
    all_gather x1, blocking collectives, body(): grouped_rows = lax.all_gather(rounded, 'fsdp', axis=0, tiled=True)  8.08 us
  transfers between devices with their start and end apart: 7, of which 6 were waited for; matrix products, arithmetic and copies ran while one was open for 0% of the time, Pallas kernels for 0%

profile of v1, /device:TPU:12, one launch (start us, length us, event | category | flops | bytes accessed | tf_op | source)
XLA Modules:
  0.0 120.3 jit_solution(10499193968160432412)
XLA Ops:
  0.6 0.0 copy-start.3
  0.7 0.6 copy-done.3
  1.3 1.0 fusion.2
  2.3 41.5 %all-reduce = f32[96,128]{1,0:T(8,128)S(1)} all-reduce(bf16[96,128]{1,0:T(8,128)(2,1)S(1)} %get-tuple-element.10), channel_id=2, replica_groups=mesh['dp'=8,'fsdp'=4] {'dp','fsdp'}, use_global_device_ids=true, to_apply=%region_0.0.clone | all-reduce | flops 12288 | bytes 73728
  43.8 0.0 copy-start.2
  43.8 0.0 copy-start.1
  43.9 0.0 copy-start
  43.9 0.1 dynamic_slice.7
  43.9 0.6 copy-done.2
  44.5 0.0 copy-done.1
  44.5 0.0 copy-done
  44.5 0.7 convert_bitcast_fusion
  45.2 8.1 %all-gather = bf16[4,3,128]{2,1,0:T(4,128)(2,1)S(1)} all-gather(bf16[1,3,128]{2,1,0:T(4,128)(2,1)S(1)} %get-tuple-element.5), channel_id=1, replica_groups=mesh['dp'=8,'fsdp'=4] {'fsdp'}, dimensions={0}, use_global_device_ids=true | all-gather | bytes 3840 | tf_op jit(solution)/shard_map/all_gather | solution.py:47
  53.3 0.0 collective-permute-start
  53.3 3.9 %collective-permute-done = bf16[12,128]{1,0:T(8,128)(2,1)S(1)} collective-permute-done((bf16[12,128]{1,0:T(8,128)(2,1)S(1)}, bf16[12,128]{1,0:T(8,128)(2,1)S(1)}, u32[]{:S(2)}, u32[]{:S(2)}) %collective-permute-start) | collective-permute-done | bytes 3104 | tf_op jit(solution)/shard_map/ppermute | solution.py:50
  57.2 0.0 collective-permute-start.1
  57.2 3.9 %collective-permute-done.1 = bf16[12,128]{1,0:T(8,128)(2,1)S(1)} collective-permute-done((bf16[12,128]{1,0:T(8,128)(2,1)S(1)}, bf16[12,128]{1,0:T(8,128)(2,1)S(1)}, u32[]{:S(2)}, u32[]{:S(2)}) %collective-permute-start.1) | collective-permute-done | bytes 3104 | tf_op jit(solution)/shard_map/ppermute | solution.py:50
  61.2 0.0 collective-permute-start.2
  61.2 3.9 %collective-permute-done.2 = bf16[12,128]{1,0:T(8,128)(2,1)S(1)} collective-permute-done((bf16[12,128]{1,0:T(8,128)(2,1)S(1)}, bf16[12,128]{1,0:T(8,128)(2,1)S(1)}, u32[]{:S(2)}, u32[]{:S(2)}) %collective-permute-start.2) | collective-permute-done | bytes 3104 | tf_op jit(solution)/shard_map/ppermute | solution.py:50
  65.1 0.0 collective-permute-start.3
  65.1 3.9 %collective-permute-done.3 = bf16[12,128]{1,0:T(8,128)(2,1)S(1)} collective-permute-done((bf16[12,128]{1,0:T(8,128)(2,1)S(1)}, bf16[12,128]{1,0:T(8,128)(2,1)S(1)}, u32[]{:S(2)}, u32[]{:S(2)}) %collective-permute-start.3) | collective-permute-done | bytes 3104 | tf_op jit(solution)/shard_map/ppermute | solution.py:50
  69.0 0.0 collective-permute-start.4
  69.0 3.9 %collective-permute-done.4 = bf16[12,128]{1,0:T(8,128)(2,1)S(1)} collective-permute-done((bf16[12,128]{1,0:T(8,128)(2,1)S(1)}, bf16[12,128]{1,0:T(8,128)(2,1)S(1)}, u32[]{:S(2)}, u32[]{:S(2)}) %collective-permute-start.4) | collective-permute-done | bytes 3104 | tf_op jit(solution)/shard_map/ppermute | solution.py:50
  73.0 0.0 collective-permute-start.5
  73.0 3.9 %collective-permute-done.5 = bf16[12,128]{1,0:T(8,128)(2,1)S(1)} collective-permute-done((bf16[12,128]{1,0:T(8,128)(2,1)S(1)}, bf16[12,128]{1,0:T(8,128)(2,1)S(1)}, u32[]{:S(2)}, u32[]{:S(2)}) %collective-permute-start.5) | collective-permute-done | bytes 3104 | tf_op jit(solution)/shard_map/ppermute | solution.py:50
  76.9 0.0 collective-permute-start.6
  76.9 41.8 %pmax.7 = f32[96]{0:T(128)} all-reduce(f32[96]{0:T(128)S(1)} %get-tuple-element.9), channel_id=1, replica_groups=mesh['dp'=8,'fsdp'=4] {'dp','fsdp'}, use_global_device_ids=true, to_apply=%region_2.3 | all-reduce | flops 96 | bytes 768 | tf_op jit(solution)/shard_map/pmax | solution.py:34
  118.7 0.0 collective-permute-done.6
  118.7 0.9 concatenate.6
  119.7 0.6 constant_dynamic-slice_fusion
  (2 shorter events, 0.0 us)
Async XLA Ops:
  0.6 0.7 copy-start.3
  43.8 0.7 copy-start.2
  43.8 0.7 copy-start.1
  43.9 0.7 copy-start
  53.3 3.9 %collective-permute-start = (bf16[12,128]{1,0:T(8,128)(2,1)S(1)}, bf16[12,128]{1,0:T(8,128)(2,1)S(1)}, u32[]{:S(2)}, u32[]{:S(2)}) collective-permute-start(bf16[12,128]{1,0:T(8,128)(2,1)S(1)} %reshape.13), channel_id=1, source_target_pairs={{0,4},{4,8},{8,12},{12,16},{16,20},{20,24},{24,28},{28,0},{1,5},{5... | collective-permute-start | bytes 9224 | tf_op jit(solution)/shard_map/ppermute | solution.py:50
  57.2 3.9 %collective-permute-start.1 = (bf16[12,128]{1,0:T(8,128)(2,1)S(1)}, bf16[12,128]{1,0:T(8,128)(2,1)S(1)}, u32[]{:S(2)}, u32[]{:S(2)}) collective-permute-start(bf16[12,128]{1,0:T(8,128)(2,1)S(1)} %collective-permute-done), channel_id=1, source_target_pairs={{0,4},{4,8},{8,12},{12,16},{16,20},{20,24},{24,28},{28,0},{1,5},{5... | collective-permute-start | bytes 9224 | tf_op jit(solution)/shard_map/ppermute | solution.py:50
  61.2 3.9 %collective-permute-start.2 = (bf16[12,128]{1,0:T(8,128)(2,1)S(1)}, bf16[12,128]{1,0:T(8,128)(2,1)S(1)}, u32[]{:S(2)}, u32[]{:S(2)}) collective-permute-start(bf16[12,128]{1,0:T(8,128)(2,1)S(1)} %collective-permute-done.1), channel_id=1, source_target_pairs={{0,4},{4,8},{8,12},{12,16},{16,20},{20,24},{24,28},{28,0},{1,5},{5... | collective-permute-start | bytes 9224 | tf_op jit(solution)/shard_map/ppermute | solution.py:50
  65.1 3.9 %collective-permute-start.3 = (bf16[12,128]{1,0:T(8,128)(2,1)S(1)}, bf16[12,128]{1,0:T(8,128)(2,1)S(1)}, u32[]{:S(2)}, u32[]{:S(2)}) collective-permute-start(bf16[12,128]{1,0:T(8,128)(2,1)S(1)} %collective-permute-done.2), channel_id=1, source_target_pairs={{0,4},{4,8},{8,12},{12,16},{16,20},{20,24},{24,28},{28,0},{1,5},{5... | collective-permute-start | bytes 9224 | tf_op jit(solution)/shard_map/ppermute | solution.py:50
  69.0 3.9 %collective-permute-start.4 = (bf16[12,128]{1,0:T(8,128)(2,1)S(1)}, bf16[12,128]{1,0:T(8,128)(2,1)S(1)}, u32[]{:S(2)}, u32[]{:S(2)}) collective-permute-start(bf16[12,128]{1,0:T(8,128)(2,1)S(1)} %collective-permute-done.3), channel_id=1, source_target_pairs={{0,4},{4,8},{8,12},{12,16},{16,20},{20,24},{24,28},{28,0},{1,5},{5... | collective-permute-start | bytes 9224 | tf_op jit(solution)/shard_map/ppermute | solution.py:50
  73.0 3.9 %collective-permute-start.5 = (bf16[12,128]{1,0:T(8,128)(2,1)S(1)}, bf16[12,128]{1,0:T(8,128)(2,1)S(1)}, u32[]{:S(2)}, u32[]{:S(2)}) collective-permute-start(bf16[12,128]{1,0:T(8,128)(2,1)S(1)} %collective-permute-done.4), channel_id=1, source_target_pairs={{0,4},{4,8},{8,12},{12,16},{16,20},{20,24},{24,28},{28,0},{1,5},{5... | collective-permute-start | bytes 9224 | tf_op jit(solution)/shard_map/ppermute | solution.py:50
  76.9 41.8 %collective-permute-start.6 = (bf16[12,128]{1,0:T(8,128)(2,1)S(1)}, bf16[12,128]{1,0:T(8,128)(2,1)S(1)}, u32[]{:S(2)}, u32[]{:S(2)}) collective-permute-start(bf16[12,128]{1,0:T(8,128)(2,1)S(1)} %collective-permute-done.5), channel_id=1, source_target_pairs={{0,4},{4,8},{8,12},{12,16},{16,20},{20,24},{24,28},{28,0},{1,5},{5... | collective-permute-start | bytes 9224 | tf_op jit(solution)/shard_map/ppermute | solution.py:50
